TPU v7x, 32 devices: a whole 2x2x4 slice. The times are simulated.
32 devices in a mesh: node: 8 (over z, x), expert: 4 (over y, core).
Axes of the slice: x: 2, y: 2, z: 4, core: 2. Of those that a mesh axis runs over, the one named last changes fastest.
Arguments:
- tokens: bfloat16 [16384, 1024], P(('node', 'expert')), may hold values from -6 to 6
- queries: bfloat16 [16384, 1024], P(('node', 'expert')), may hold values from -6 to 6
- keys: bfloat16 [16384, 1024], P(('node', 'expert')), may hold values from -6 to 6
- values: bfloat16 [16384, 1024], P(('node', 'expert')), may hold values from -12 to 12
- neighbours: int32 [128, 8], P(('node', 'expert')), may hold values from 0 to 127, as said below
- live_bits: int32 [128, 8], P(('node', 'expert')), may hold values from 0 to 1, as said below
- out_proj: bfloat16 [1024, 1024], replicated, may hold values from -0.1875 to 0.1875
- norm_gain: float32 [1024], replicated, may hold values from 0.5 to 1.5
- router: bfloat16 [1024, 32], replicated, may hold values from -0.1875 to 0.1875
- expert: int32 [16384], P(('node', 'expert')), may hold values from 0 to 31, as said below
- slot: int32 [16384], P(('node', 'expert')), may hold values from 0 to 31, as said below
- w_up: bfloat16 [32, 1024, 4096], P(('node', 'expert')), may hold values from -0.1875 to 0.1875
- w_down: bfloat16 [32, 4096, 1024], P(('node', 'expert')), may hold values from -0.09375 to 0.09375
Outputs:
- layer_out: bfloat16 [16384, 1024], P(('node', 'expert'))
Inputs may be any that keep to these rules, and one draw needn't show every extreme that they name: Tile g is held by device g // 4 in node-major order. neighbours[g, 0] is g itself; every listed tile is held by g's device or by the device one step before or after it along node with the same expert index (wrapping around); entry 1 is always one step before and entry 2 one step after. `live_bits`: entry 0 of every row is 1. Within the 512 tokens of one device, no two tokens share both expert and slot; some expert takes all 32 slots of every device. See expert: pairs (expert, slot) are distinct within one device's tokens.
All inputs are finite; a program needn't handle non-finite values.
Results may differ from a plain program's by a relative error of at most 0.0049.
Values may be sent and summed in bfloat16 or wider, within the bound.
A program may use at most 192 MiB of HBM per device.

v0:
```python
import functools

import jax
import jax.numpy as jnp
from jax import lax
from jax.experimental import pallas as pl
from jax.experimental.pallas import tpu as pltpu
from jax.sharding import PartitionSpec as P

D = 1024
HEADS = 16
HEAD_DIM = 64
TILE = 128
NB = 8


score_scale = 0.125


CHUNKS = 4
HIDE = -1e30
STACK = 2


def attention_kernel(
    nodes,
    position_ref,
    bias_ref,
    query_hbm,
    key_ref,
    value_ref,
    token_hbm,
    proj_hbm,
    gain_ref,
    hidden_ref,
    normed_ref,
    *scratch,
):
    key_windows, value_windows = scratch[:CHUNKS], scratch[CHUNKS : 2 * CHUNKS]
    own_sem, x_send, x_recv, z_send, z_recv, attn_ref = scratch[2 * CHUNKS : 2 * CHUNKS + 6]
    query_ref, token_ref, proj_ref, load_sem = scratch[2 * CHUNKS + 6 :]
    token_load = pltpu.make_async_copy(token_hbm, token_ref, load_sem.at[0])
    query_load = pltpu.make_async_copy(query_hbm, query_ref, load_sem.at[1])
    proj_load = pltpu.make_async_copy(proj_hbm, proj_ref, load_sem.at[2])
    node = lax.axis_index("node")
    odd = node % 2
    partner = node + 1 - 2 * odd
    onward = (node + 2 - 4 * odd + nodes) % nodes
    behind = (node - 2 + 4 * odd + nodes) % nodes
    tiles = key_windows[0].shape[0] // 3
    width = key_windows[0].shape[2]
    barrier = pltpu.get_barrier_semaphore()
    for other in (partner, onward, behind):
        pl.semaphore_signal(
            barrier, inc=1, device_id={"node": other}, device_id_type=pl.DeviceIdType.MESH
        )
    pl.semaphore_wait(barrier, 3)
    own, first, second = [], [], []
    for c in range(CHUNKS):
        columns = pl.ds(c * width, width)
        for s, (source, window) in enumerate(
            ((key_ref, key_windows[c]), (value_ref, value_windows[c]))
        ):
            block = source.at[:, :, columns]
            own.append(
                pltpu.make_async_copy(block, window.at[pl.ds(0, tiles)], own_sem.at[2 * c + s])
            )
            first.append(
                pltpu.make_async_remote_copy(
                    src_ref=block,
                    dst_ref=window.at[pl.ds(tiles, tiles)],
                    send_sem=x_send.at[2 * c + s],
                    recv_sem=x_recv.at[2 * c + s],
                    device_id={"node": partner},
                    device_id_type=pl.DeviceIdType.MESH,
                )
            )
            second.append(
                pltpu.make_async_remote_copy(
                    src_ref=window.at[pl.ds(tiles, tiles)],
                    dst_ref=window.at[pl.ds(2 * tiles, tiles)],
                    send_sem=z_send.at[2 * c + s],
                    recv_sem=z_recv.at[2 * c + s],
                    device_id={"node": onward},
                    device_id_type=pl.DeviceIdType.MESH,
                )
            )
    for copy in first:
        copy.start()
    for copy in own + [token_load, query_load, proj_load]:
        copy.start()
    token_load.wait()
    hidden_ref[...] = token_ref[...].astype(jnp.float32)
    heads = width // HEAD_DIM
    lane_head = lax.broadcasted_iota(jnp.int32, (TILE, width), 1) // HEAD_DIM

    def relay(c):
        for s in range(2):
            first[2 * c + s].wait_recv()
            second[2 * c + s].start()

    def attend(c):
        def one_tile(t, carry):
            rows = pl.ds(pl.multiple_of(t * TILE, TILE), TILE)
            query = query_ref[rows, c * width : (c + 1) * width] * jnp.bfloat16(score_scale)
            near_keys = jnp.concatenate(
                [key_windows[c][position_ref[t, j]] for j in range(NB)], axis=0
            )
            near_values = jnp.concatenate(
                [value_windows[c][position_ref[t, j]] for j in range(NB)], axis=0
            )
            bias = bias_ref[t]
            mixed = jnp.zeros((TILE, width), jnp.float32)
            for h in range(0, heads, STACK):
                mine = jnp.concatenate(
                    [
                        jnp.where(lane_head == h + i, query, jnp.zeros_like(query))
                        for i in range(STACK)
                    ],
                    axis=0,
                )
                scores = lax.dot_general(
                    mine,
                    near_keys,
                    (((1,), (1,)), ((), ())),
                    preferred_element_type=jnp.float32,
                )
                scores = scores + bias
                peak = jnp.max(scores, axis=-1, keepdims=True)
                weights = jnp.exp(scores - peak)
                share = 1.0 / jnp.sum(weights, axis=-1, keepdims=True)
                weights = (weights * share).astype(jnp.bfloat16)
                out = jnp.dot(weights, near_values, preferred_element_type=jnp.float32)
                for i in range(STACK):
                    mixed = jnp.where(lane_head == h + i, out[i * TILE : (i + 1) * TILE], mixed)
            attn_ref[rows, :] = mixed.astype(jnp.bfloat16)
            return carry

        lax.fori_loop(0, tiles, one_tile, 0)

        def project(t, carry):
            rows = pl.ds(pl.multiple_of(t * TILE, TILE), TILE)
            hidden_ref[rows, :] += jnp.dot(
                attn_ref[rows, :],
                proj_ref[c * width : (c + 1) * width, :],
                preferred_element_type=jnp.float32,
            )
            return carry

        lax.fori_loop(0, tiles, project, 0)

    query_load.wait()
    proj_load.wait()
    relay(0)
    for c in range(CHUNKS):
        if c + 1 < CHUNKS:
            relay(c + 1)
        for s in range(2):
            own[2 * c + s].wait()
            second[2 * c + s].wait_recv()
        attend(c)

    def finish(t, carry):
        rows = pl.ds(pl.multiple_of(t * TILE, TILE), TILE)
        hidden = hidden_ref[rows, :]
        spread = jnp.mean(hidden * hidden, axis=-1, keepdims=True)
        normed = hidden * lax.rsqrt(spread + 1e-06) * gain_ref[...]
        normed_ref[rows, :] = normed.astype(jnp.bfloat16)
        return carry

    lax.fori_loop(0, tiles, finish, 0)
    for copy in first + second:
        copy.wait_send()


def attention_block(tokens, queries, keys, values, position, live_bits, out_proj, norm_gain):
    tok_dev = tokens.shape[0]
    tiles = tok_dev // TILE
    width = D // CHUNKS
    bias = jnp.where(jnp.repeat(live_bits, TILE, axis=1) > 0, 0.0, HIDE).astype(jnp.float32)
    window = pltpu.VMEM((3 * tiles, TILE, width), jnp.bfloat16)
    sems = pltpu.SemaphoreType.DMA((2 * CHUNKS,))
    vmem = pl.BlockSpec(memory_space=pltpu.VMEM)
    anywhere = pl.BlockSpec(memory_space=pl.ANY)
    return pl.pallas_call(
        functools.partial(attention_kernel, lax.axis_size("node")),
        out_shape=(
            jax.ShapeDtypeStruct((tok_dev, D), jnp.float32),
            jax.ShapeDtypeStruct((tok_dev, D), jnp.bfloat16),
        ),
        in_specs=[
            pl.BlockSpec(memory_space=pltpu.SMEM),
            vmem,
            anywhere,
            anywhere,
            anywhere,
            anywhere,
            anywhere,
            vmem,
        ],
        out_specs=(vmem, vmem),
        scratch_shapes=[window] * (2 * CHUNKS)
        + [sems] * 5
        + [
            pltpu.VMEM((tok_dev, width), jnp.bfloat16),
            pltpu.VMEM((tok_dev, D), jnp.bfloat16),
            pltpu.VMEM((tok_dev, D), jnp.bfloat16),
            pltpu.VMEM((D, D), jnp.bfloat16),
            pltpu.SemaphoreType.DMA((3,)),
        ],
        compiler_params=pltpu.CompilerParams(
            collective_id=0, has_side_effects=True, vmem_limit_bytes=62 * 1024 * 1024
        ),
    )(
        position,
        bias.reshape(tiles, 1, NB * TILE),
        queries,
        keys.reshape(tiles, TILE, D),
        values.reshape(tiles, TILE, D),
        tokens,
        out_proj,
        norm_gain.reshape(1, D),
    )


GROUPS = 4
SPAN = 512


def expert_kernel(
    nodes, columns, outgoing_ref, up_ref, down_ref, back_ref, *scratch
):
    (
        rows_ref,
        result_ref,
        up_held,
        down_held,
        total_ref,
        weight_sem,
        own_sem,
        there_send,
        there_recv,
        back_send,
        back_recv,
    ) = scratch
    devices = nodes * columns
    cap = outgoing_ref.shape[1]
    members = devices // GROUPS
    me = lax.axis_index("node") * columns + lax.axis_index("expert")
    up_copy = pltpu.make_async_copy(up_ref.at[0], up_held, weight_sem.at[0])
    down_copy = pltpu.make_async_copy(down_ref.at[0], down_held, weight_sem.at[1])

    def place(device):
        return {"node": device // columns, "expert": device % columns}

    barrier = pltpu.get_barrier_semaphore()

    def greet(k, carry):
        pl.semaphore_signal(
            barrier,
            inc=1,
            device_id=place((me + k) % devices),
            device_id_type=pl.DeviceIdType.MESH,
        )
        return carry

    lax.fori_loop(1, devices, greet, 0)
    pl.semaphore_wait(barrier, devices - 1)

    def block(g, j):
        return pl.ds(pl.multiple_of(j * cap, cap), cap)

    def there(i):
        g, j = i // members, i % members
        target = (me + g + GROUPS * j) % devices
        return pltpu.make_async_remote_copy(
            src_ref=outgoing_ref.at[target],
            dst_ref=rows_ref.at[g, block(g, j)],
            send_sem=there_send.at[i],
            recv_sem=there_recv.at[i],
            device_id=place(target),
            device_id_type=pl.DeviceIdType.MESH,
        )

    def back(i):
        g, j = i // members, i % members
        target = (me + devices - g - GROUPS * j) % devices
        return pltpu.make_async_remote_copy(
            src_ref=result_ref.at[g, block(g, j)],
            dst_ref=back_ref.at[me],
            send_sem=back_send.at[i],
            recv_sem=back_recv.at[i],
            device_id=place(target),
            device_id_type=pl.DeviceIdType.MESH,
        )

    def back_from(i):
        g, j = i // members, i % members
        source = (me + g + GROUPS * j) % devices
        return pltpu.make_async_remote_copy(
            src_ref=result_ref.at[g, block(g, j)],
            dst_ref=back_ref.at[source],
            send_sem=back_send.at[i],
            recv_sem=back_recv.at[i],
            device_id=place(source),
            device_id_type=pl.DeviceIdType.MESH,
        )

    def each(lower, upper, act):
        def step(i, carry):
            act(i)
            return carry

        lax.fori_loop(lower, upper, step, 0)

    each(1, devices, lambda i: there(i).start())
    up_copy.start()
    down_copy.start()
    own_rows = pltpu.make_async_copy(
        outgoing_ref.at[me], rows_ref.at[0, pl.ds(0, cap)], own_sem.at[0]
    )
    own_rows.start()
    own_back = pltpu.make_async_copy(
        result_ref.at[0, pl.ds(0, cap)], back_ref.at[me], own_sem.at[1]
    )
    spans = up_held.shape[1] // SPAN
    for g in range(GROUPS):
        first = max(g * members, 1)
        each(first, (g + 1) * members, lambda i: there(i).wait_recv())
        if g == 0:
            own_rows.wait()
            up_copy.wait()
            down_copy.wait()

        def span(f, carry, g=g):
            part = pl.ds(pl.multiple_of(f * SPAN, SPAN), SPAN)
            lifted = jnp.dot(rows_ref[g], up_held[:, part], preferred_element_type=jnp.float32)
            lifted = jax.nn.gelu(lifted, approximate=True).astype(jnp.bfloat16)
            total_ref[...] += jnp.dot(
                lifted, down_held[part, :], preferred_element_type=jnp.float32
            )
            return carry

        total_ref[...] = jnp.zeros_like(total_ref)
        lax.fori_loop(0, spans, span, 0)
        result_ref[g] = total_ref[...].astype(jnp.bfloat16)
        if g == 0:
            own_back.start()
        each(first, (g + 1) * members, lambda i: back(i).start())
    own_back.wait()
    each(1, devices, lambda i: there(i).wait_send())
    each(1, devices, lambda i: back(i).wait_send())
    each(1, devices, lambda i: back_from(i).wait_recv())


def expert_exchange(outgoing, w_up, w_down):
    devices, cap, _ = outgoing.shape
    hidden_units = w_up.shape[2]
    rows = devices // GROUPS * cap
    anywhere = pl.BlockSpec(memory_space=pl.ANY)
    sems = pltpu.SemaphoreType.DMA((devices,))
    pair = pltpu.SemaphoreType.DMA((2,))
    return pl.pallas_call(
        functools.partial(expert_kernel, lax.axis_size("node"), lax.axis_size("expert")),
        out_shape=jax.ShapeDtypeStruct(outgoing.shape, jnp.bfloat16),
        in_specs=[anywhere] * 3,
        out_specs=anywhere,
        scratch_shapes=[
            pltpu.VMEM((GROUPS, rows, D), jnp.bfloat16),
            pltpu.VMEM((GROUPS, rows, D), jnp.bfloat16),
            pltpu.VMEM((D, hidden_units), jnp.bfloat16),
            pltpu.VMEM((hidden_units, D), jnp.bfloat16),
            pltpu.VMEM((rows, D), jnp.float32),
            pair,
            pair,
            sems,
            sems,
            sems,
            sems,
        ],
        compiler_params=pltpu.CompilerParams(
            collective_id=1, has_side_effects=True, vmem_limit_bytes=62 * 1024 * 1024
        ),
    )(outgoing, w_up, w_down)


def exchange_by_blocks(outgoing, w_up, w_down):
    experts, cap, _ = outgoing.shape
    block = lax.all_to_all(
        outgoing.reshape(experts, 1, cap, D),
        ("node", "expert"),
        split_axis=0,
        concat_axis=1,
        tiled=True,
    )
    token_rows = block.reshape(-1, D)
    lifted = jnp.dot(token_rows, w_up[0], preferred_element_type=jnp.float32)
    lifted = jax.nn.gelu(lifted, approximate=True).astype(jnp.bfloat16)
    result = jnp.dot(lifted, w_down[0], preferred_element_type=jnp.float32).astype(jnp.bfloat16)
    return lax.all_to_all(
        result.reshape(block.shape), ("node", "expert"), split_axis=1, concat_axis=0, tiled=True
    )


def shards(
    tokens,
    queries,
    keys,
    values,
    neighbours,
    live_bits,
    out_proj,
    norm_gain,
    router,
    expert,
    slot,
    w_up,
    w_down,
):
    tok_dev = tokens.shape[0]
    tiles_dev = tok_dev // TILE
    experts = router.shape[1]
    cap = 2 * tok_dev // experts
    my_node = lax.axis_index("node")
    column_count = lax.axis_size("expert")
    owner_node = neighbours // tiles_dev // column_count
    partner = my_node + 1 - 2 * (my_node % 2)
    block_of = jnp.where(owner_node == my_node, 0, jnp.where(owner_node == partner, 1, 2))
    position = block_of * tiles_dev + neighbours % tiles_dev
    hidden, normed = attention_block(
        tokens, queries, keys, values, position, live_bits, out_proj, norm_gain
    )
    logits = jnp.dot(normed, router, preferred_element_type=jnp.float32)
    columns = lax.iota(jnp.int32, experts)
    chosen = jnp.sum(jnp.where(columns[None, :] == expert[:, None], logits, 0.0), axis=-1)
    gate = jax.nn.sigmoid(chosen)
    slot_cell = expert * cap + slot
    one_hot = (lax.iota(jnp.int32, experts * cap)[:, None] == slot_cell[None, :]).astype(
        jnp.bfloat16
    )
    outgoing = jnp.dot(one_hot, normed, preferred_element_type=jnp.float32).astype(jnp.bfloat16)
    exchange = exchange_by_blocks if cap % 16 else expert_exchange
    returned = exchange(outgoing.reshape(experts, cap, D), w_up, w_down)
    flat_back = returned.reshape(experts * cap, D)
    expert_out = jnp.einsum("ct,cd->td", one_hot, flat_back, preferred_element_type=jnp.float32)
    layer_out = hidden + gate[:, None] * expert_out
    return layer_out.astype(jnp.bfloat16)


def solution(mesh):
    in_specs = (
        P(("node", "expert"), None),
        P(("node", "expert"), None),
        P(("node", "expert"), None),
        P(("node", "expert"), None),
        P(("node", "expert"), None),
        P(("node", "expert"), None),
        P(),
        P(),
        P(),
        P(("node", "expert")),
        P(("node", "expert")),
        P(("node", "expert"), None, None),
        P(("node", "expert"), None, None),
    )
    out_specs = P(("node", "expert"), None)
    return jax.shard_map(shards, mesh=mesh, in_specs=in_specs, out_specs=out_specs, check_vma=False)
```

profile of v0, /device:TPU:0, one launch (start us, length us, event | category | flops | bytes accessed | tf_op | source)
XLA Modules:
  0.0 179.8 jit_solution(13316737139598363191)
XLA Ops:
  0.0 0.0 copy-start
  0.0 1.3 fusion.7.position_ref
  1.3 0.7 multiply_add_fusion
  2.0 0.7 compare_select_fusion
  2.7 0.7 broadcast_in_dim.28
  3.4 0.0 copy-start.1
  3.4 69.0 %shard_map.127 = (f32[512,1024]{1,0:T(8,128)}, bf16[512,1024]{1,0:T(8,128)(2,1)}) custom-call(s32[4,8]{1,0:T(4,128)} %fusion.7.position_ref, f32[4,1,1024]{2,1,0:T(1,128)} %bitcast.14, bf16[512,1024]{1,0:T(8,128)(2,1)} %query_hbm.1, bf16[4,128,1024]{2,1,0:T(8,128)(2,1)} %bitcast.12, bf16[4,128,1024]{2,1,0:T(8,128)(2,1)} %bitcast.13, ...), custom_call_target="tpu_custom_call" | custom-call | tf_op jit(solution)/shard_map/pallas_call | solution.py:185
  72.4 0.0 copy-done
  72.4 0.0 copy-done.1
  72.4 1.7 fusion.3
  74.1 3.8 %fusion.2 = bf16[1024,1024]{1,0:T(8,128)(2,1)} fusion(bf16[512,1024]{1,0:T(8,128)(2,1)} %get-tuple-element.8, s32[512]{0:T(512)S(1)} %multiply_add_fusion), kind=kOutput, calls=%fused_computation.4 | convolution fusion | flops 1075314688 | bytes 3147776 | tf_op jit(solution)/shard_map/dot_general | solution.py:441
  77.8 97.4 %shard_map.128 = bf16[32,32,1024]{2,1,0:T(8,128)(2,1)} custom-call(bf16[32,32,1024]{2,1,0:T(8,128)(2,1)} %bitcast.11, bf16[1,1024,4096]{2,1,0:T(8,128)(2,1)} %up_ref.1, bf16[1,4096,1024]{2,1,0:T(8,128)(2,1)} %down_ref.1), custom_call_target="tpu_custom_call" | custom-call | tf_op jit(solution)/shard_map/pallas_call | solution.py:363
  175.3 4.5 %add_convert_fusion = bf16[512,1024]{1,0:T(8,128)(2,1)} fusion(f32[512,1024]{1,0:T(8,128)} %get-tuple-element.7, bf16[1024,1024]{1,0:T(8,128)(2,1)} %bitcast.10, s32[512]{0:T(512)S(1)} %multiply_add_fusion, f32[512]{0:T(512)S(1)} %add_divide_fusion), kind=kOutput, calls=%fused_computation | convolution fusion | flops 1075838976 | bytes 5246976 | tf_op jit(solution)/shard_map/ct,cd->td/dot_general | solution.py:445
  (1 shorter events, 0.0 us)
Async XLA Ops:
  0.0 72.4 %copy-start = (bf16[1024,32]{0,1:T(8,128)(2,1)S(1)}, bf16[1024,32]{0,1:T(8,128)(2,1)}, u32[]{:S(2)}) copy-start(bf16[1024,32]{0,1:T(8,128)(2,1)} %param.21) | copy-start | bytes 196612
  3.4 69.0 %copy-start.1 = (s32[512]{0:T(512)S(1)}, s32[512]{0:T(512)}, u32[]{:S(2)}) copy-start(s32[512]{0:T(512)} %param.22) | copy-start | bytes 6148
where the time goes:
time: 180 us
  Pallas kernels  166 us (92%)
  matrix products  9.95 us (6%)
  other arithmetic  2.7 us (2%)
    pallas_call x1, Pallas kernels, expert_exchange(): pl.pallas_call(functools.partial(expert_kernel, lax.axis_size('node'), la...  97.4 us
    pallas_call x1, Pallas kernels, attention_block(): pl.pallas_call(functools.partial(attention_kernel, lax.axis_size('node'))...  69 us
    dot_general x1, matrix products, shards(): jnp.einsum('ct,cd->td', one_hot, flat_back, preferred_element_type=jnp.fl...  4.5 us
    dot_general x1, matrix products, shards(): jnp.dot(one_hot, normed, preferred_element_type=jnp.float32)  3.79 us

commit v1 on v0

--- a/solution.py
+++ b/solution.py
@@ -17,51 +17,78 @@
 score_scale = 0.125
 
 
-CHUNKS = 4
+LANES = 128
 HIDE = -1e30
-STACK = 2
 
 
 def attention_kernel(
     nodes,
-    position_ref,
-    bias_ref,
+    columns,
+    neighbour_ref,
+    live_ref,
     query_hbm,
     key_ref,
     value_ref,
     token_hbm,
     proj_hbm,
+    router_ref,
     gain_ref,
+    expert_ref,
     hidden_ref,
     normed_ref,
+    gate_ref,
+    level_ref,
     *scratch,
 ):
-    key_windows, value_windows = scratch[:CHUNKS], scratch[CHUNKS : 2 * CHUNKS]
-    own_sem, x_send, x_recv, z_send, z_recv, attn_ref = scratch[2 * CHUNKS : 2 * CHUNKS + 6]
-    query_ref, token_ref, proj_ref, load_sem = scratch[2 * CHUNKS + 6 :]
+    chunks = D // LANES
+    key_windows, value_windows = scratch[:chunks], scratch[chunks : 2 * chunks]
+    own_sem, x_send, x_recv, z_send, z_recv, attn_ref = scratch[2 * chunks : 2 * chunks + 6]
+    query_ref, token_ref, proj_ref, load_sem = scratch[2 * chunks + 6 : 2 * chunks + 10]
+    bias_ref, weight_ref, count_ref, peers_ref, level_send, level_recv = scratch[2 * chunks + 10 :]
+    devices = nodes * columns
     token_load = pltpu.make_async_copy(token_hbm, token_ref, load_sem.at[0])
-    query_load = pltpu.make_async_copy(query_hbm, query_ref, load_sem.at[1])
-    proj_load = pltpu.make_async_copy(proj_hbm, proj_ref, load_sem.at[2])
+    proj_load = pltpu.make_async_copy(proj_hbm, proj_ref, load_sem.at[1])
+    query_load = pltpu.make_async_copy(query_hbm, query_ref, load_sem.at[2])
     node = lax.axis_index("node")
+    me = node * columns + lax.axis_index("expert")
     odd = node % 2
     partner = node + 1 - 2 * odd
     onward = (node + 2 - 4 * odd + nodes) % nodes
-    behind = (node - 2 + 4 * odd + nodes) % nodes
     tiles = key_windows[0].shape[0] // 3
-    width = key_windows[0].shape[2]
     barrier = pltpu.get_barrier_semaphore()
-    for other in (partner, onward, behind):
+
+    def place(device):
+        return {"node": device // columns, "expert": device % columns}
+
+    def greet(k, carry):
         pl.semaphore_signal(
-            barrier, inc=1, device_id={"node": other}, device_id_type=pl.DeviceIdType.MESH
-        )
-    pl.semaphore_wait(barrier, 3)
+            barrier,
+            inc=1,
+            device_id=place((me + k) % devices),
+            device_id_type=pl.DeviceIdType.MESH,
+        )
+        return carry
+
+    lax.fori_loop(1, devices, greet, 0)
+
+    members = devices // GROUPS
+    plane = me // members
+    away = (expert_ref[...] // members - plane + GROUPS) % GROUPS
+    most = jnp.zeros((1, 1), jnp.float32)
+    for g in range(1, GROUPS):
+        most = jnp.maximum(
+            most, jnp.sum(jnp.where(away == g, 1.0, 0.0), axis=1, keepdims=True)
+        )
+    count_ref[...] = jnp.broadcast_to(most, count_ref.shape)
+    peers_ref[me] = jnp.broadcast_to(most, count_ref.shape)
+
     own, first, second = [], [], []
-    for c in range(CHUNKS):
-        columns = pl.ds(c * width, width)
+    for c in range(chunks):
+        lanes = pl.ds(c * LANES, LANES)
         for s, (source, window) in enumerate(
             ((key_ref, key_windows[c]), (value_ref, value_windows[c]))
         ):
-            block = source.at[:, :, columns]
+            block = source.at[:, :, lanes]
             own.append(
                 pltpu.make_async_copy(block, window.at[pl.ds(0, tiles)], own_sem.at[2 * c + s])
             )
@@ -85,146 +112,191 @@
                     device_id_type=pl.DeviceIdType.MESH,
                 )
             )
+
+    def tell(k, source):
+        return pltpu.make_async_remote_copy(
+            src_ref=count_ref,
+            dst_ref=peers_ref.at[source],
+            send_sem=level_send.at[k],
+            recv_sem=level_recv.at[k],
+            device_id=place((me + k) % devices),
+            device_id_type=pl.DeviceIdType.MESH,
+        )
+
+    def each_peer(act):
+        def step(k, carry):
+            act(k)
+            return carry
+
+        lax.fori_loop(1, devices, step, 0)
+
+    pl.semaphore_wait(barrier, devices - 1)
     for copy in first:
         copy.start()
     for copy in own + [token_load, query_load, proj_load]:
         copy.start()
+    each_peer(lambda k: tell(k, me).start())
+    for t in range(tiles):
+        for j in range(NB):
+            hide = jnp.where(live_ref[t, j] > 0, 0.0, HIDE)
+            bias_ref[t, j * TILE : (j + 1) * TILE, :] = jnp.full(
+                (TILE, LANES), hide, jnp.float32
+            ).astype(jnp.bfloat16)
     token_load.wait()
     hidden_ref[...] = token_ref[...].astype(jnp.float32)
-    heads = width // HEAD_DIM
-    lane_head = lax.broadcasted_iota(jnp.int32, (TILE, width), 1) // HEAD_DIM
-
-    def relay(c):
-        for s in range(2):
-            first[2 * c + s].wait_recv()
-            second[2 * c + s].start()
-
-    def attend(c):
-        def one_tile(t, carry):
-            rows = pl.ds(pl.multiple_of(t * TILE, TILE), TILE)
-            query = query_ref[rows, c * width : (c + 1) * width] * jnp.bfloat16(score_scale)
-            near_keys = jnp.concatenate(
-                [key_windows[c][position_ref[t, j]] for j in range(NB)], axis=0
-            )
-            near_values = jnp.concatenate(
-                [value_windows[c][position_ref[t, j]] for j in range(NB)], axis=0
-            )
-            bias = bias_ref[t]
-            mixed = jnp.zeros((TILE, width), jnp.float32)
-            for h in range(0, heads, STACK):
-                mine = jnp.concatenate(
-                    [
-                        jnp.where(lane_head == h + i, query, jnp.zeros_like(query))
-                        for i in range(STACK)
-                    ],
-                    axis=0,
-                )
-                scores = lax.dot_general(
-                    mine,
-                    near_keys,
-                    (((1,), (1,)), ((), ())),
-                    preferred_element_type=jnp.float32,
-                )
-                scores = scores + bias
-                peak = jnp.max(scores, axis=-1, keepdims=True)
-                weights = jnp.exp(scores - peak)
-                share = 1.0 / jnp.sum(weights, axis=-1, keepdims=True)
-                weights = (weights * share).astype(jnp.bfloat16)
-                out = jnp.dot(weights, near_values, preferred_element_type=jnp.float32)
-                for i in range(STACK):
-                    mixed = jnp.where(lane_head == h + i, out[i * TILE : (i + 1) * TILE], mixed)
-            attn_ref[rows, :] = mixed.astype(jnp.bfloat16)
-            return carry
-
-        lax.fori_loop(0, tiles, one_tile, 0)
-
-        def project(t, carry):
-            rows = pl.ds(pl.multiple_of(t * TILE, TILE), TILE)
-            hidden_ref[rows, :] += jnp.dot(
-                attn_ref[rows, :],
-                proj_ref[c * width : (c + 1) * width, :],
-                preferred_element_type=jnp.float32,
-            )
-            return carry
-
-        lax.fori_loop(0, tiles, project, 0)
+    lane = lax.broadcasted_iota(jnp.int32, (TILE, LANES), 1)
+    low = lane < HEAD_DIM
+    mark = (lax.broadcasted_iota(jnp.int32, (2 * TILE, LANES), 1) == 0).astype(jnp.bfloat16)
+    ones = jnp.ones((NB * TILE, LANES), jnp.bfloat16)
+
+    def position(t, j):
+        listed = neighbour_ref[t, j]
+        owner = listed // (tiles * columns)
+        block = jnp.where(owner == node, 0, jnp.where(owner == partner, 1, 2))
+        return block * tiles + listed % tiles
+
+    def scores_of(c, t):
+        query = query_ref[t * TILE : (t + 1) * TILE, c * LANES : (c + 1) * LANES]
+        query = query * jnp.bfloat16(score_scale)
+        blank = jnp.zeros_like(query)
+        mine = jnp.concatenate(
+            [jnp.where(low, query, blank), jnp.where(low, blank, query)], axis=0
+        )
+        near_keys = jnp.concatenate(
+            [key_windows[c][position(t, j)] for j in range(NB)], axis=0
+        )
+        scores = lax.dot_general(
+            jnp.concatenate([mine, mark], axis=1),
+            jnp.concatenate([near_keys, bias_ref[t]], axis=1),
+            (((1,), (1,)), ((), ())),
+            preferred_element_type=jnp.float32,
+        )
+        peak = jnp.max(scores, axis=-1, keepdims=True)
+        weight_ref[t] = jnp.exp(scores - peak).astype(jnp.bfloat16)
+
+    def values_of(c, t):
+        near_values = jnp.concatenate(
+            [value_windows[c][position(t, j)] for j in range(NB)], axis=0
+        )
+        out = jnp.dot(
+            weight_ref[t],
+            jnp.concatenate([near_values, ones], axis=1),
+            preferred_element_type=jnp.float32,
+        )
+        share = out[:, :LANES] / out[:, LANES:]
+        attn_ref[t * TILE : (t + 1) * TILE, :] = jnp.where(
+            low, share[:TILE], share[TILE:]
+        ).astype(jnp.bfloat16)
+
+    def relay(i):
+        if i < 2 * chunks:
+            first[i].wait_recv()
+            second[i].start()
 
     query_load.wait()
     proj_load.wait()
     relay(0)
-    for c in range(CHUNKS):
-        if c + 1 < CHUNKS:
-            relay(c + 1)
-        for s in range(2):
-            own[2 * c + s].wait()
-            second[2 * c + s].wait_recv()
-        attend(c)
+    for c in range(chunks):
+        relay(2 * c + 1)
+        own[2 * c].wait()
+        second[2 * c].wait_recv()
+        for t in range(tiles):
+            scores_of(c, t)
+        relay(2 * c + 2)
+        own[2 * c + 1].wait()
+        if c == chunks - 1:
+            each_peer(lambda k: tell(k, (me - k + devices) % devices).wait_recv())
+            level_ref[...] = jnp.max(peers_ref[...], axis=0)
+            for copy in first:
+                copy.wait_send()
+            each_peer(lambda k: tell(k, me).wait_send())
+        second[2 * c + 1].wait_recv()
+        for t in range(tiles):
+            values_of(c, t)
+        hidden_ref[...] += jnp.dot(
+            attn_ref[...],
+            proj_ref[c * LANES : (c + 1) * LANES, :],
+            preferred_element_type=jnp.float32,
+        )
 
     def finish(t, carry):
         rows = pl.ds(pl.multiple_of(t * TILE, TILE), TILE)
         hidden = hidden_ref[rows, :]
         spread = jnp.mean(hidden * hidden, axis=-1, keepdims=True)
-        normed = hidden * lax.rsqrt(spread + 1e-06) * gain_ref[...]
-        normed_ref[rows, :] = normed.astype(jnp.bfloat16)
+        normed = (hidden * lax.rsqrt(spread + 1e-06) * gain_ref[...]).astype(jnp.bfloat16)
+        normed_ref[rows, :] = normed
+        logits = jnp.dot(normed, router_ref[...], preferred_element_type=jnp.float32)
+        experts = logits.shape[1]
+        wanted = jnp.transpose(
+            jnp.broadcast_to(expert_ref[:, rows].astype(jnp.float32), (TILE, TILE))
+        )[:, :experts]
+        column = lax.broadcasted_iota(jnp.int32, (TILE, experts), 1).astype(jnp.float32)
+        chosen = jnp.sum(jnp.where(wanted == column, logits, 0.0), axis=-1, keepdims=True)
+        gate_ref[rows, :] = jnp.broadcast_to(jax.nn.sigmoid(chosen), (TILE, LANES))
         return carry
 
     lax.fori_loop(0, tiles, finish, 0)
-    for copy in first + second:
+    for copy in second:
         copy.wait_send()
 
 
-def attention_block(tokens, queries, keys, values, position, live_bits, out_proj, norm_gain):
+def attention_block(
+    tokens, queries, keys, values, neighbours, live_bits, out_proj, norm_gain, router, expert
+):
     tok_dev = tokens.shape[0]
     tiles = tok_dev // TILE
-    width = D // CHUNKS
-    bias = jnp.where(jnp.repeat(live_bits, TILE, axis=1) > 0, 0.0, HIDE).astype(jnp.float32)
-    window = pltpu.VMEM((3 * tiles, TILE, width), jnp.bfloat16)
-    sems = pltpu.SemaphoreType.DMA((2 * CHUNKS,))
+    chunks = D // LANES
+    devices = lax.axis_size("node") * lax.axis_size("expert")
+    window = pltpu.VMEM((3 * tiles, TILE, LANES), jnp.bfloat16)
+    sems = pltpu.SemaphoreType.DMA((2 * chunks,))
     vmem = pl.BlockSpec(memory_space=pltpu.VMEM)
+    smem = pl.BlockSpec(memory_space=pltpu.SMEM)
     anywhere = pl.BlockSpec(memory_space=pl.ANY)
     return pl.pallas_call(
-        functools.partial(attention_kernel, lax.axis_size("node")),
+        functools.partial(attention_kernel, lax.axis_size("node"), lax.axis_size("expert")),
         out_shape=(
             jax.ShapeDtypeStruct((tok_dev, D), jnp.float32),
             jax.ShapeDtypeStruct((tok_dev, D), jnp.bfloat16),
+            jax.ShapeDtypeStruct((tok_dev, LANES), jnp.float32),
+            jax.ShapeDtypeStruct((8, LANES), jnp.float32),
         ),
-        in_specs=[
-            pl.BlockSpec(memory_space=pltpu.SMEM),
-            vmem,
-            anywhere,
-            anywhere,
-            anywhere,
-            anywhere,
-            anywhere,
-            vmem,
-        ],
-        out_specs=(vmem, vmem),
-        scratch_shapes=[window] * (2 * CHUNKS)
+        in_specs=[smem, smem] + [anywhere] * 5 + [vmem] * 3,
+        out_specs=(vmem,) * 4,
+        scratch_shapes=[window] * (2 * chunks)
         + [sems] * 5
         + [
-            pltpu.VMEM((tok_dev, width), jnp.bfloat16),
+            pltpu.VMEM((tok_dev, LANES), jnp.bfloat16),
             pltpu.VMEM((tok_dev, D), jnp.bfloat16),
             pltpu.VMEM((tok_dev, D), jnp.bfloat16),
             pltpu.VMEM((D, D), jnp.bfloat16),
             pltpu.SemaphoreType.DMA((3,)),
+            pltpu.VMEM((tiles, NB * TILE, LANES), jnp.bfloat16),
+            pltpu.VMEM((tiles, 2 * TILE, NB * TILE), jnp.bfloat16),
+            pltpu.VMEM((8, LANES), jnp.float32),
+            pltpu.VMEM((devices, 8, LANES), jnp.float32),
+            pltpu.SemaphoreType.DMA((devices,)),
+            pltpu.SemaphoreType.DMA((devices,)),
         ],
         compiler_params=pltpu.CompilerParams(
             collective_id=0, has_side_effects=True, vmem_limit_bytes=62 * 1024 * 1024
         ),
     )(
-        position,
-        bias.reshape(tiles, 1, NB * TILE),
+        neighbours,
+        live_bits,
         queries,
         keys.reshape(tiles, TILE, D),
         values.reshape(tiles, TILE, D),
         tokens,
         out_proj,
+        router,
         norm_gain.reshape(1, D),
+        expert.reshape(1, tok_dev),
     )
 
 
 GROUPS = 4
 SPAN = 512
+ORDER = (2, 1, 3)
 
 
 def expert_kernel(
@@ -384,6 +456,312 @@
     )(outgoing, w_up, w_down)
 
 
+def relay_kernel(
+    nodes,
+    columns,
+    normed_ref,
+    hidden_hbm,
+    gate_ref,
+    expert_ref,
+    slot_ref,
+    up_ref,
+    down_ref,
+    out_ref,
+    up_held,
+    down_held,
+    hidden_ref,
+    total_ref,
+    mixed_ref,
+    packed_ref,
+    guide_ref,
+    taken_ref,
+    taken_guide_ref,
+    padded_ref,
+    rows_ref,
+    result_ref,
+    back_ref,
+    repacked_ref,
+    home_ref,
+    load_sem,
+    hop_send,
+    hop_recv,
+    guide_send,
+    guide_recv,
+    home_send,
+    home_recv,
+    there_send,
+    there_recv,
+    back_send,
+    back_recv,
+):
+    devices = nodes * columns
+    members = devices // GROUPS
+    tok_dev = normed_ref.shape[0]
+    fit = packed_ref.shape[1]
+    block = rows_ref.shape[1] // members
+    cells = members * block
+    me = lax.axis_index("node") * columns + lax.axis_index("expert")
+    plane, member = me // members, me % members
+    up_copy = pltpu.make_async_copy(up_ref.at[0], up_held, load_sem.at[0])
+    down_copy = pltpu.make_async_copy(down_ref.at[0], down_held, load_sem.at[1])
+    hidden_copy = pltpu.make_async_copy(hidden_hbm, hidden_ref, load_sem.at[2])
+
+    def place(device):
+        return {"node": device // columns, "expert": device % columns}
+
+    def mate(g):
+        return place((plane + g) % GROUPS * members + member)
+
+    def peer(k):
+        return place(plane * members + (member + k) % members)
+
+    barrier = pltpu.get_barrier_semaphore()
+    for target in [mate(g) for g in range(1, GROUPS)] + [peer(k) for k in range(1, members)]:
+        pl.semaphore_signal(
+            barrier, inc=1, device_id=target, device_id_type=pl.DeviceIdType.MESH
+        )
+    up_copy.start()
+    down_copy.start()
+    hidden_copy.start()
+
+    away = (expert_ref[...] // members - plane + GROUPS) % GROUPS
+    cell = expert_ref[...] % members * block + slot_ref[...]
+    lines = lax.broadcasted_iota(jnp.int32, (8, tok_dev), 0)
+    earlier = (
+        lax.broadcasted_iota(jnp.int32, (tok_dev, tok_dev), 0)
+        < lax.broadcasted_iota(jnp.int32, (tok_dev, tok_dev), 1)
+    ).astype(jnp.bfloat16)
+    ranks = jnp.dot(
+        (lines == away).astype(jnp.bfloat16), earlier, preferred_element_type=jnp.float32
+    ).astype(jnp.int32)
+    cell_lines = jnp.broadcast_to((cell + 1).astype(jnp.float32), (8, tok_dev)).astype(
+        jnp.bfloat16
+    )
+    seats = [jnp.where(away == 0, cell, -1)] + [
+        jnp.where(away == g, ranks[g : g + 1, :], -1) for g in range(1, GROUPS)
+    ]
+
+    def spread(g, count):
+        return (lax.broadcasted_iota(jnp.int32, (count, tok_dev), 0) == seats[g]).astype(
+            jnp.bfloat16
+        )
+
+    def hop(g):
+        return pltpu.make_async_remote_copy(
+            src_ref=packed_ref.at[g - 1],
+            dst_ref=taken_ref.at[g - 1],
+            send_sem=hop_send.at[g],
+            recv_sem=hop_recv.at[g],
+            device_id=mate(g),
+            device_id_type=pl.DeviceIdType.MESH,
+        )
+
+    def guide(g):
+        return pltpu.make_async_remote_copy(
+            src_ref=guide_ref.at[g - 1],
+            dst_ref=taken_guide_ref.at[g - 1],
+            send_sem=guide_send.at[g],
+            recv_sem=guide_recv.at[g],
+            device_id=mate(g),
+            device_id_type=pl.DeviceIdType.MESH,
+        )
+
+    def homeward(g):
+        return pltpu.make_async_remote_copy(
+            src_ref=repacked_ref.at[g - 1],
+            dst_ref=home_ref.at[g - 1],
+            send_sem=home_send.at[g],
+            recv_sem=home_recv.at[g],
+            device_id=mate(GROUPS - g),
+            device_id_type=pl.DeviceIdType.MESH,
+        )
+
+    def part(k):
+        return pl.ds(pl.multiple_of(k % members * block, block), block)
+
+    def there(g, k, source):
+        return pltpu.make_async_remote_copy(
+            src_ref=padded_ref.at[g, part(member + k)],
+            dst_ref=rows_ref.at[g, part(source)],
+            send_sem=there_send.at[g, k],
+            recv_sem=there_recv.at[g, k],
+            device_id=peer(k),
+            device_id_type=pl.DeviceIdType.MESH,
+        )
+
+    def back(g, k, source):
+        return pltpu.make_async_remote_copy(
+            src_ref=result_ref.at[g, part(member + k)],
+            dst_ref=back_ref.at[g, part(source)],
+            send_sem=back_send.at[g, k],
+            recv_sem=back_recv.at[g, k],
+            device_id=peer(k),
+            device_id_type=pl.DeviceIdType.MESH,
+        )
+
+    def each(act):
+        def step(k, carry):
+            act(k)
+            return carry
+
+        lax.fori_loop(1, members, step, 0)
+
+    def hand_out(g):
+        each(lambda k: there(g, k, member).start())
+        rows_ref[g, part(member), :] = padded_ref[g, part(member), :]
+
+    def placing(g):
+        return (
+            lax.broadcasted_iota(jnp.int32, (cells, fit), 0).astype(jnp.float32) + 1.0
+            == taken_guide_ref[g - 1, 0:1, :]
+        ).astype(jnp.bfloat16)
+
+    def expand(g):
+        guide(g).wait_recv()
+        hop(g).wait_recv()
+        padded_ref[g] = jnp.dot(
+            placing(g), taken_ref[g - 1], preferred_element_type=jnp.float32
+        ).astype(jnp.bfloat16)
+        hand_out(g)
+
+    def compute(g):
+        each(lambda k: there(g, k, member + members - k).wait_recv())
+
+        def span(f, carry):
+            columns_f = pl.ds(pl.multiple_of(f * SPAN, SPAN), SPAN)
+            lifted = jnp.dot(
+                rows_ref[g], up_held[:, columns_f], preferred_element_type=jnp.float32
+            )
+            lifted = jax.nn.gelu(lifted, approximate=True).astype(jnp.bfloat16)
+            total_ref[...] += jnp.dot(
+                lifted, down_held[columns_f, :], preferred_element_type=jnp.float32
+            )
+            return carry
+
+        total_ref[...] = jnp.zeros_like(total_ref)
+        lax.fori_loop(0, up_held.shape[1] // SPAN, span, 0)
+        result_ref[g] = total_ref[...].astype(jnp.bfloat16)
+        each(lambda k: back(g, k, member).start())
+        back_ref[g, part(member), :] = result_ref[g, part(member), :]
+
+    def collect(g):
+        each(lambda k: back(g, k, member + members - k).wait_recv())
+
+    def repack(g):
+        collect(g)
+        repacked_ref[g - 1] = lax.dot_general(
+            placing(g),
+            back_ref[g],
+            (((0,), (0,)), ((), ())),
+            preferred_element_type=jnp.float32,
+        ).astype(jnp.bfloat16)
+        homeward(g).start()
+
+    def take_home(g, source, count):
+        seated = spread(g, count)
+        return lax.dot_general(
+            seated, source, (((0,), (0,)), ((), ())), preferred_element_type=jnp.float32
+        )
+
+    for g in ORDER:
+        seated = spread(g, fit)
+        packed_ref[g - 1] = jnp.dot(
+            seated, normed_ref[...], preferred_element_type=jnp.float32
+        ).astype(jnp.bfloat16)
+        guide_ref[g - 1] = lax.dot_general(
+            cell_lines, seated, (((1,), (1,)), ((), ())), preferred_element_type=jnp.float32
+        )
+        if g == ORDER[0]:
+            pl.semaphore_wait(barrier, GROUPS + members - 2)
+        guide(g).start()
+        hop(g).start()
+    padded_ref[0] = jnp.dot(
+        spread(0, cells), normed_ref[...], preferred_element_type=jnp.float32
+    ).astype(jnp.bfloat16)
+    hand_out(0)
+    up_copy.wait()
+    down_copy.wait()
+    compute(0)
+    one, two, three = ORDER
+    expand(one)
+    collect(0)
+    mixed_ref[...] = take_home(0, back_ref[0], cells)
+    expand(two)
+    compute(one)
+    compute(two)
+    expand(three)
+    repack(one)
+    repack(two)
+    compute(three)
+    repack(three)
+    hidden_copy.wait()
+    for g in ORDER[:-1]:
+        homeward(g).wait_recv()
+        mixed_ref[...] += take_home(g, home_ref[g - 1], fit)
+    homeward(three).wait_recv()
+    mixed = mixed_ref[...] + take_home(three, home_ref[three - 1], fit)
+    out_ref[...] = (hidden_ref[...] + gate_ref[:, 0:1] * mixed).astype(jnp.bfloat16)
+    for g in range(GROUPS):
+        each(lambda k: there(g, k, member).wait_send())
+        each(lambda k: back(g, k, member).wait_send())
+    for g in ORDER:
+        guide(g).wait_send()
+        hop(g).wait_send()
+        homeward(g).wait_send()
+
+
+def relay_exchange(fit, normed, hidden, gate, expert, slot, w_up, w_down):
+    tok_dev = normed.shape[0]
+    hidden_units = w_up.shape[2]
+    nodes, columns = lax.axis_size("node"), lax.axis_size("expert")
+    members = nodes * columns // GROUPS
+    cells = 2 * tok_dev // GROUPS
+    anywhere = pl.BlockSpec(memory_space=pl.ANY)
+    vmem = pl.BlockSpec(memory_space=pltpu.VMEM)
+    packed = pltpu.VMEM((GROUPS - 1, fit, D), jnp.bfloat16)
+    guides = pltpu.VMEM((GROUPS - 1, 8, fit), jnp.float32)
+    grouped = pltpu.VMEM((GROUPS, cells, D), jnp.bfloat16)
+    hop_sems = pltpu.SemaphoreType.DMA((GROUPS,))
+    peer_sems = pltpu.SemaphoreType.DMA((GROUPS, members))
+    return pl.pallas_call(
+        functools.partial(relay_kernel, nodes, columns),
+        out_shape=jax.ShapeDtypeStruct((tok_dev, D), jnp.bfloat16),
+        in_specs=[vmem, anywhere, vmem, vmem, vmem, anywhere, anywhere],
+        out_specs=vmem,
+        scratch_shapes=[
+            pltpu.VMEM((D, hidden_units), jnp.bfloat16),
+            pltpu.VMEM((hidden_units, D), jnp.bfloat16),
+            pltpu.VMEM((tok_dev, D), jnp.float32),
+            pltpu.VMEM((cells, D), jnp.float32),
+            pltpu.VMEM((tok_dev, D), jnp.float32),
+            packed,
+            guides,
+            packed,
+            guides,
+            grouped,
+            grouped,
+            grouped,
+            grouped,
+            packed,
+            packed,
+            pltpu.SemaphoreType.DMA((3,)),
+        ]
+        + [hop_sems] * 6
+        + [peer_sems] * 4,
+        compiler_params=pltpu.CompilerParams(
+            collective_id=2, has_side_effects=True, vmem_limit_bytes=62 * 1024 * 1024
+        ),
+    )(
+        normed,
+        hidden,
+        gate,
+        expert.reshape(1, tok_dev),
+        slot.reshape(1, tok_dev),
+        w_up,
+        w_down,
+    )
+
+
 def exchange_by_blocks(outgoing, w_up, w_down):
     experts, cap, _ = outgoing.shape
     block = lax.all_to_all(
@@ -418,33 +796,36 @@
     w_down,
 ):
     tok_dev = tokens.shape[0]
-    tiles_dev = tok_dev // TILE
     experts = router.shape[1]
     cap = 2 * tok_dev // experts
-    my_node = lax.axis_index("node")
-    column_count = lax.axis_size("expert")
-    owner_node = neighbours // tiles_dev // column_count
-    partner = my_node + 1 - 2 * (my_node % 2)
-    block_of = jnp.where(owner_node == my_node, 0, jnp.where(owner_node == partner, 1, 2))
-    position = block_of * tiles_dev + neighbours % tiles_dev
-    hidden, normed = attention_block(
-        tokens, queries, keys, values, position, live_bits, out_proj, norm_gain
+    hidden, normed, gate, level = attention_block(
+        tokens, queries, keys, values, neighbours, live_bits, out_proj, norm_gain, router, expert
     )
-    logits = jnp.dot(normed, router, preferred_element_type=jnp.float32)
-    columns = lax.iota(jnp.int32, experts)
-    chosen = jnp.sum(jnp.where(columns[None, :] == expert[:, None], logits, 0.0), axis=-1)
-    gate = jax.nn.sigmoid(chosen)
-    slot_cell = expert * cap + slot
-    one_hot = (lax.iota(jnp.int32, experts * cap)[:, None] == slot_cell[None, :]).astype(
-        jnp.bfloat16
-    )
-    outgoing = jnp.dot(one_hot, normed, preferred_element_type=jnp.float32).astype(jnp.bfloat16)
-    exchange = exchange_by_blocks if cap % 16 else expert_exchange
-    returned = exchange(outgoing.reshape(experts, cap, D), w_up, w_down)
-    flat_back = returned.reshape(experts * cap, D)
-    expert_out = jnp.einsum("ct,cd->td", one_hot, flat_back, preferred_element_type=jnp.float32)
-    layer_out = hidden + gate[:, None] * expert_out
-    return layer_out.astype(jnp.bfloat16)
+
+    def padded_way():
+        slot_cell = expert * cap + slot
+        one_hot = (lax.iota(jnp.int32, experts * cap)[:, None] == slot_cell[None, :]).astype(
+            jnp.bfloat16
+        )
+        outgoing = jnp.dot(one_hot, normed, preferred_element_type=jnp.float32).astype(
+            jnp.bfloat16
+        )
+        exchange = exchange_by_blocks if cap % 16 else expert_exchange
+        returned = exchange(outgoing.reshape(experts, cap, D), w_up, w_down)
+        flat_back = returned.reshape(experts * cap, D)
+        expert_out = jnp.einsum(
+            "ct,cd->td", one_hot, flat_back, preferred_element_type=jnp.float32
+        )
+        layer_out = hidden + gate[:, :1] * expert_out
+        return layer_out.astype(jnp.bfloat16)
+
+    def relayed_way():
+        return relay_exchange(fit, normed, hidden, gate, expert, slot, w_up, w_down)
+
+    fit = 2 * tok_dev // GROUPS * 3 // 4
+    if cap % 16 or lax.axis_size("node") % GROUPS:
+        return padded_way()
+    return lax.cond(level[0, 0] <= fit, relayed_way, padded_way)
 
 
 def solution(mesh):

time: 180 us -> 167 us (0.928)
  the two profiles are of different devices: /device:TPU:0 before, /device:TPU:13 now
where the time goes in v1:
time: 167 us
  Pallas kernels  161 us (96%)
  local copies, waits for them, and re-layouts  5.15 us (3%)
    pallas_call x1, Pallas kernels, relay_exchange(): pl.pallas_call(functools.partial(relay_kernel, nodes, columns), out_shape...  99.1 us
    pallas_call x1, Pallas kernels, attention_block(): pl.pallas_call(functools.partial(attention_kernel, lax.axis_size('node'),...  61.9 us
    unnamed x6, local copies, waits for them, and re-layouts  3.95 us

profile of v1, /device:TPU:13, one launch (start us, length us, event | category | flops | bytes accessed | tf_op | source)
XLA Modules:
  0.0 166.9 jit_solution(911285657083580241)
XLA Ops:
  0.0 1.7 %copy.17.router_ref = bf16[1024,32]{1,0:T(8,128)(2,1)} copy(bf16[1024,32]{0,1:T(8,128)(2,1)} %param.23) | data formatting | bytes 131072 | tf_op args[8]
  1.7 0.0 copy-start
  1.7 0.0 copy-start.1
  1.7 61.9 %shard_map.129 = (f32[512,1024]{1,0:T(8,128)}, bf16[512,1024]{1,0:T(8,128)(2,1)S(1)}, f32[512,128]{1,0:T(8,128)S(1)}, f32[8,128]{1,0:T(8,128)}) custom-call(s32[4,8]{1,0:T(4,128)} %neighbour_ref.1, s32[4,8]{1,0:T(4,128)} %live_ref.1, bf16[512,1024]{1,0:T(8,128)(2,1)} %query_hbm.1, bf16[4,128,1024]{2,1,0:T(8,128)(2,1)} %bitcast.14, ...), custom_call_target="tpu_custom_call" | custom-call | tf_op jit(solution)/shard_map/pallas_call | solution.py:255
  63.6 1.2 slice.6
  65.5 0.0 copy-done
  65.5 0.0 copy-done.1
  65.5 99.1 %conditional.1 = (bf16[512,1024]{1,0:T(8,128)(2,1)}) conditional(s32[]{:T(128)} %bitcast.9, (f32[512,128]{1,0:T(8,128)S(1)}, s32[512]{0:T(512)S(1)}, s32[512]{0:T(512)S(1)}, bf16[512,1024]{1,0:T(8,128)(2,1)S(1)}, bf16[1,1024,4096]{2,1,0:T(8,128)(2,1)}, /*index=5*/bf16[1,4096,1024]{2,1,0:T(8,128)(2,1)}, f32[512,1024]{1,0:T(8,128)}) %tuple.20, ...), branch_computations={%region_0.0_spmd, %region_1.0_spmd} | conditional | flops 2151154688 | bytes 8929288 | solution.py:828
  65.5 99.1 %branch_1_fun.1 = bf16[512,1024]{1,0:T(8,128)(2,1)} custom-call(bf16[512,1024]{1,0:T(8,128)(2,1)S(1)} %get-tuple-element.43.normed_ref, f32[512,1024]{1,0:T(8,128)} %get-tuple-element.44.hidden_hbm, f32[512,128]{1,0:T(8,128)S(1)} %get-tuple-element.45.gate_ref, s32[1,512]{1,0:T(1,128)S(1)} %bitcast.17, s32[1,512]{1,0:T(1,128)S(1)} %bitcast.18, ...), custom_call_target="tpu_custom_call" | custom-call | tf_op jit(solution)/shard_map/cond/branch_1_fun/pallas_call | solution.py:726
  164.6 2.3 %copy.22 = bf16[512,1024]{1,0:T(8,128)(2,1)} copy(bf16[512,1024]{1,0:T(8,128)(2,1)} %get-tuple-element.58) | data formatting | bytes 2097152
Async XLA Ops:
  1.7 63.8 %copy-start = (s32[512]{0:T(512)S(1)}, s32[512]{0:T(512)}, u32[]{:S(2)}) copy-start(s32[512]{0:T(512)} %param.24) | copy-start | bytes 6148
  1.7 63.8 %copy-start.1 = (s32[512]{0:T(512)S(1)}, s32[512]{0:T(512)}, u32[]{:S(2)}) copy-start(s32[512]{0:T(512)} %param.25) | copy-start | bytes 6148

commit v2 on v1

--- a/solution.py
+++ b/solution.py
@@ -18,6 +18,18 @@
 
 
 LANES = 128
+GROUPS = 4
+RELAYED = (2, 3)
+
+
+def across(plane, g):
+    if g % 2:
+        plane = plane + 1 - 2 * (plane % 2)
+    if g // 2:
+        plane = plane + 2 - 4 * (plane // 2)
+    return plane
+
+
 HIDE = -1e30
 
 
@@ -73,12 +85,11 @@
 
     members = devices // GROUPS
     plane = me // members
-    away = (expert_ref[...] // members - plane + GROUPS) % GROUPS
+    wanted_plane = expert_ref[...] // members
     most = jnp.zeros((1, 1), jnp.float32)
-    for g in range(1, GROUPS):
-        most = jnp.maximum(
-            most, jnp.sum(jnp.where(away == g, 1.0, 0.0), axis=1, keepdims=True)
-        )
+    for g in RELAYED:
+        there = jnp.where(wanted_plane == across(plane, g), 1.0, 0.0)
+        most = jnp.maximum(most, jnp.sum(there, axis=1, keepdims=True))
     count_ref[...] = jnp.broadcast_to(most, count_ref.shape)
     peers_ref[me] = jnp.broadcast_to(most, count_ref.shape)
 
@@ -201,8 +212,9 @@
         own[2 * c].wait()
         second[2 * c].wait_recv()
         for t in range(tiles):
+            if t == tiles - 1:
+                relay(2 * c + 2)
             scores_of(c, t)
-        relay(2 * c + 2)
         own[2 * c + 1].wait()
         if c == chunks - 1:
             each_peer(lambda k: tell(k, (me - k + devices) % devices).wait_recv())
@@ -225,7 +237,12 @@
         spread = jnp.mean(hidden * hidden, axis=-1, keepdims=True)
         normed = (hidden * lax.rsqrt(spread + 1e-06) * gain_ref[...]).astype(jnp.bfloat16)
         normed_ref[rows, :] = normed
-        logits = jnp.dot(normed, router_ref[...], preferred_element_type=jnp.float32)
+        logits = lax.dot_general(
+            normed,
+            router_ref[...],
+            (((1,), (1,)), ((), ())),
+            preferred_element_type=jnp.float32,
+        )
         experts = logits.shape[1]
         wanted = jnp.transpose(
             jnp.broadcast_to(expert_ref[:, rows].astype(jnp.float32), (TILE, TILE))
@@ -288,15 +305,13 @@
         values.reshape(tiles, TILE, D),
         tokens,
         out_proj,
-        router,
+        router.T,
         norm_gain.reshape(1, D),
         expert.reshape(1, tok_dev),
     )
 
 
-GROUPS = 4
-SPAN = 512
-ORDER = (2, 1, 3)
+SPAN = 256
 
 
 def expert_kernel(
@@ -396,29 +411,31 @@
         result_ref.at[0, pl.ds(0, cap)], back_ref.at[me], own_sem.at[1]
     )
     spans = up_held.shape[1] // SPAN
-    for g in range(GROUPS):
-        first = max(g * members, 1)
+    own_rows.wait()
+    up_copy.wait()
+    down_copy.wait()
+
+    def group(g, carry):
+        first = jnp.maximum(g * members, 1)
         each(first, (g + 1) * members, lambda i: there(i).wait_recv())
-        if g == 0:
-            own_rows.wait()
-            up_copy.wait()
-            down_copy.wait()
-
-        def span(f, carry, g=g):
+
+        def span(f, inner):
             part = pl.ds(pl.multiple_of(f * SPAN, SPAN), SPAN)
             lifted = jnp.dot(rows_ref[g], up_held[:, part], preferred_element_type=jnp.float32)
             lifted = jax.nn.gelu(lifted, approximate=True).astype(jnp.bfloat16)
             total_ref[...] += jnp.dot(
                 lifted, down_held[part, :], preferred_element_type=jnp.float32
             )
-            return carry
+            return inner
 
         total_ref[...] = jnp.zeros_like(total_ref)
         lax.fori_loop(0, spans, span, 0)
         result_ref[g] = total_ref[...].astype(jnp.bfloat16)
-        if g == 0:
-            own_back.start()
         each(first, (g + 1) * members, lambda i: back(i).start())
+        return carry
+
+    lax.fori_loop(0, GROUPS, group, 0)
+    own_back.start()
     own_back.wait()
     each(1, devices, lambda i: there(i).wait_send())
     each(1, devices, lambda i: back(i).wait_send())
@@ -456,6 +473,9 @@
     )(outgoing, w_up, w_down)
 
 
+WIDE = 512
+
+
 def relay_kernel(
     nodes,
     columns,
@@ -471,6 +491,7 @@
     down_held,
     hidden_ref,
     total_ref,
+    lifted_ref,
     mixed_ref,
     packed_ref,
     guide_ref,
@@ -509,14 +530,17 @@
     def place(device):
         return {"node": device // columns, "expert": device % columns}
 
+    def member_of(g, j):
+        return place(across(plane, g) * members + j % members)
+
     def mate(g):
-        return place((plane + g) % GROUPS * members + member)
-
-    def peer(k):
-        return place(plane * members + (member + k) % members)
+        return member_of(g, member)
 
     barrier = pltpu.get_barrier_semaphore()
-    for target in [mate(g) for g in range(1, GROUPS)] + [peer(k) for k in range(1, members)]:
+    greeted = [mate(g) for g in RELAYED]
+    greeted += [member_of(0, member + k) for k in range(1, members)]
+    greeted += [member_of(1, member + k) for k in range(members)]
+    for target in greeted:
         pl.semaphore_signal(
             barrier, inc=1, device_id=target, device_id_type=pl.DeviceIdType.MESH
         )
@@ -524,7 +548,7 @@
     down_copy.start()
     hidden_copy.start()
 
-    away = (expert_ref[...] // members - plane + GROUPS) % GROUPS
+    wanted = expert_ref[...] // members
     cell = expert_ref[...] % members * block + slot_ref[...]
     lines = lax.broadcasted_iota(jnp.int32, (8, tok_dev), 0)
     earlier = (
@@ -532,13 +556,19 @@
         < lax.broadcasted_iota(jnp.int32, (tok_dev, tok_dev), 1)
     ).astype(jnp.bfloat16)
     ranks = jnp.dot(
-        (lines == away).astype(jnp.bfloat16), earlier, preferred_element_type=jnp.float32
+        (
+            ((lines == RELAYED[0]) & (wanted == across(plane, RELAYED[0])))
+            | ((lines == RELAYED[1]) & (wanted == across(plane, RELAYED[1])))
+        ).astype(jnp.bfloat16),
+        earlier,
+        preferred_element_type=jnp.float32,
     ).astype(jnp.int32)
     cell_lines = jnp.broadcast_to((cell + 1).astype(jnp.float32), (8, tok_dev)).astype(
         jnp.bfloat16
     )
-    seats = [jnp.where(away == 0, cell, -1)] + [
-        jnp.where(away == g, ranks[g : g + 1, :], -1) for g in range(1, GROUPS)
+    seats = [
+        jnp.where(wanted == across(plane, g), ranks[g : g + 1, :] if g in RELAYED else cell, -1)
+        for g in range(GROUPS)
     ]
 
     def spread(g, count):
@@ -548,8 +578,8 @@
 
     def hop(g):
         return pltpu.make_async_remote_copy(
-            src_ref=packed_ref.at[g - 1],
-            dst_ref=taken_ref.at[g - 1],
+            src_ref=packed_ref.at[g - 2],
+            dst_ref=taken_ref.at[g - 2],
             send_sem=hop_send.at[g],
             recv_sem=hop_recv.at[g],
             device_id=mate(g),
@@ -558,8 +588,8 @@
 
     def guide(g):
         return pltpu.make_async_remote_copy(
-            src_ref=guide_ref.at[g - 1],
-            dst_ref=taken_guide_ref.at[g - 1],
+            src_ref=guide_ref.at[g - 2],
+            dst_ref=taken_guide_ref.at[g - 2],
             send_sem=guide_send.at[g],
             recv_sem=guide_recv.at[g],
             device_id=mate(g),
@@ -568,11 +598,11 @@
 
     def homeward(g):
         return pltpu.make_async_remote_copy(
-            src_ref=repacked_ref.at[g - 1],
-            dst_ref=home_ref.at[g - 1],
+            src_ref=repacked_ref.at[g - 2],
+            dst_ref=home_ref.at[g - 2],
             send_sem=home_send.at[g],
             recv_sem=home_recv.at[g],
-            device_id=mate(GROUPS - g),
+            device_id=mate(g),
             device_id_type=pl.DeviceIdType.MESH,
         )
 
@@ -585,7 +615,7 @@
             dst_ref=rows_ref.at[g, part(source)],
             send_sem=there_send.at[g, k],
             recv_sem=there_recv.at[g, k],
-            device_id=peer(k),
+            device_id=member_of(g % 2 if g < 2 else 0, member + k),
             device_id_type=pl.DeviceIdType.MESH,
         )
 
@@ -595,61 +625,79 @@
             dst_ref=back_ref.at[g, part(source)],
             send_sem=back_send.at[g, k],
             recv_sem=back_recv.at[g, k],
-            device_id=peer(k),
-            device_id_type=pl.DeviceIdType.MESH,
-        )
-
-    def each(act):
+            device_id=member_of(g % 2 if g < 2 else 0, member + k),
+            device_id_type=pl.DeviceIdType.MESH,
+        )
+
+    def each(g, act):
         def step(k, carry):
             act(k)
             return carry
 
-        lax.fori_loop(1, members, step, 0)
+        lax.fori_loop(0 if g == 1 else 1, members, step, 0)
 
     def hand_out(g):
-        each(lambda k: there(g, k, member).start())
-        rows_ref[g, part(member), :] = padded_ref[g, part(member), :]
+        each(g, lambda k: there(g, k, member).start())
+        if g != 1:
+            rows_ref[g, part(member), :] = padded_ref[g, part(member), :]
 
     def placing(g):
         return (
             lax.broadcasted_iota(jnp.int32, (cells, fit), 0).astype(jnp.float32) + 1.0
-            == taken_guide_ref[g - 1, 0:1, :]
+            == taken_guide_ref[g - 2, 0:1, :]
         ).astype(jnp.bfloat16)
 
     def expand(g):
         guide(g).wait_recv()
         hop(g).wait_recv()
         padded_ref[g] = jnp.dot(
-            placing(g), taken_ref[g - 1], preferred_element_type=jnp.float32
+            placing(g), taken_ref[g - 2], preferred_element_type=jnp.float32
         ).astype(jnp.bfloat16)
         hand_out(g)
 
-    def compute(g):
-        each(lambda k: there(g, k, member + members - k).wait_recv())
-
-        def span(f, carry):
-            columns_f = pl.ds(pl.multiple_of(f * SPAN, SPAN), SPAN)
+    def compute(g, wide):
+        each(g, lambda k: there(g, k, member + members - k).wait_recv())
+        spans = up_held.shape[1] // wide
+
+        def lift(f, slot):
+            part_f = pl.ds(pl.multiple_of(f * wide, wide), wide)
             lifted = jnp.dot(
-                rows_ref[g], up_held[:, columns_f], preferred_element_type=jnp.float32
+                rows_ref[g], up_held[:, part_f], preferred_element_type=jnp.float32
             )
-            lifted = jax.nn.gelu(lifted, approximate=True).astype(jnp.bfloat16)
+            lifted_ref[slot, :, :wide] = jax.nn.gelu(lifted, approximate=True).astype(jnp.bfloat16)
+
+        def lower(f, slot):
+            part_f = pl.ds(pl.multiple_of(f * wide, wide), wide)
             total_ref[...] += jnp.dot(
-                lifted, down_held[columns_f, :], preferred_element_type=jnp.float32
+                lifted_ref[slot, :, :wide], down_held[part_f, :], preferred_element_type=jnp.float32
             )
+
+        def span(i, carry):
+            lift(2 * i + 1, 1)
+            lower(2 * i, 0)
+            lift(2 * i + 2, 0)
+            lower(2 * i + 1, 1)
             return carry
 
         total_ref[...] = jnp.zeros_like(total_ref)
-        lax.fori_loop(0, up_held.shape[1] // SPAN, span, 0)
+        lift(0, 0)
+        lax.fori_loop(0, spans // 2 - 1, span, 0)
+        lift(spans - 1, 1)
+        lower(spans - 2, 0)
+        lower(spans - 1, 1)
         result_ref[g] = total_ref[...].astype(jnp.bfloat16)
-        each(lambda k: back(g, k, member).start())
-        back_ref[g, part(member), :] = result_ref[g, part(member), :]
+
+    def reply(g):
+        each(g, lambda k: back(g, k, member).start())
+        if g != 1:
+            back_ref[g, part(member), :] = result_ref[g, part(member), :]
 
     def collect(g):
-        each(lambda k: back(g, k, member + members - k).wait_recv())
+        each(g, lambda k: back(g, k, member + members - k).wait_recv())
 
     def repack(g):
         collect(g)
-        repacked_ref[g - 1] = lax.dot_general(
+        repacked_ref[g - 2] = lax.dot_general(
             placing(g),
             back_ref[g],
             (((0,), (0,)), ((), ())),
@@ -663,50 +711,63 @@
             seated, source, (((0,), (0,)), ((), ())), preferred_element_type=jnp.float32
         )
 
-    for g in ORDER:
+    def pack(g):
         seated = spread(g, fit)
-        packed_ref[g - 1] = jnp.dot(
+        packed_ref[g - 2] = jnp.dot(
             seated, normed_ref[...], preferred_element_type=jnp.float32
         ).astype(jnp.bfloat16)
-        guide_ref[g - 1] = lax.dot_general(
+        guide_ref[g - 2] = lax.dot_general(
             cell_lines, seated, (((1,), (1,)), ((), ())), preferred_element_type=jnp.float32
         )
-        if g == ORDER[0]:
-            pl.semaphore_wait(barrier, GROUPS + members - 2)
-        guide(g).start()
-        hop(g).start()
-    padded_ref[0] = jnp.dot(
-        spread(0, cells), normed_ref[...], preferred_element_type=jnp.float32
-    ).astype(jnp.bfloat16)
+
+    def pad(g):
+        padded_ref[g] = jnp.dot(
+            spread(g, cells), normed_ref[...], preferred_element_type=jnp.float32
+        ).astype(jnp.bfloat16)
+
+    near, far = RELAYED
+    pad(1)
+    pl.semaphore_wait(barrier, len(greeted))
+    hand_out(1)
+    pad(0)
     hand_out(0)
+    pack(near)
+    guide(near).start()
+    hop(near).start()
+    pack(far)
     up_copy.wait()
     down_copy.wait()
-    compute(0)
-    one, two, three = ORDER
-    expand(one)
+    compute(0, WIDE // 2)
+    reply(0)
+    hop(near).wait_send()
+    guide(far).start()
+    hop(far).start()
+    expand(near)
+    compute(1, WIDE // 2)
+    reply(1)
+    compute(near, WIDE)
+    reply(near)
     collect(0)
     mixed_ref[...] = take_home(0, back_ref[0], cells)
-    expand(two)
-    compute(one)
-    compute(two)
-    expand(three)
-    repack(one)
-    repack(two)
-    compute(three)
-    repack(three)
+    expand(far)
+    collect(1)
+    mixed_ref[...] += take_home(1, back_ref[1], cells)
+    repack(near)
+    compute(far, WIDE)
+    reply(far)
+    repack(far)
     hidden_copy.wait()
-    for g in ORDER[:-1]:
-        homeward(g).wait_recv()
-        mixed_ref[...] += take_home(g, home_ref[g - 1], fit)
-    homeward(three).wait_recv()
-    mixed = mixed_ref[...] + take_home(three, home_ref[three - 1], fit)
+    homeward(near).wait_recv()
+    mixed_ref[...] += take_home(near, home_ref[near - 2], fit)
+    homeward(far).wait_recv()
+    mixed = mixed_ref[...] + take_home(far, home_ref[far - 2], fit)
     out_ref[...] = (hidden_ref[...] + gate_ref[:, 0:1] * mixed).astype(jnp.bfloat16)
     for g in range(GROUPS):
-        each(lambda k: there(g, k, member).wait_send())
-        each(lambda k: back(g, k, member).wait_send())
-    for g in ORDER:
+        each(g, lambda k: there(g, k, member).wait_send())
+        each(g, lambda k: back(g, k, member).wait_send())
+    hop(far).wait_send()
+    for g in RELAYED:
         guide(g).wait_send()
-        hop(g).wait_send()
         homeward(g).wait_send()
 
 
@@ -718,8 +779,8 @@
     cells = 2 * tok_dev // GROUPS
     anywhere = pl.BlockSpec(memory_space=pl.ANY)
     vmem = pl.BlockSpec(memory_space=pltpu.VMEM)
-    packed = pltpu.VMEM((GROUPS - 1, fit, D), jnp.bfloat16)
-    guides = pltpu.VMEM((GROUPS - 1, 8, fit), jnp.float32)
+    packed = pltpu.VMEM((len(RELAYED), fit, D), jnp.bfloat16)
+    guides = pltpu.VMEM((len(RELAYED), 8, fit), jnp.float32)
     grouped = pltpu.VMEM((GROUPS, cells, D), jnp.bfloat16)
     hop_sems = pltpu.SemaphoreType.DMA((GROUPS,))
     peer_sems = pltpu.SemaphoreType.DMA((GROUPS, members))
@@ -733,6 +794,7 @@
             pltpu.VMEM((hidden_units, D), jnp.bfloat16),
             pltpu.VMEM((tok_dev, D), jnp.float32),
             pltpu.VMEM((cells, D), jnp.float32),
+            pltpu.VMEM((2, cells, WIDE), jnp.bfloat16),
             pltpu.VMEM((tok_dev, D), jnp.float32),
             packed,
             guides,

time: 167 us -> 162 us (0.970)
  Pallas kernels: 161 us -> 158 us
  local copies, waits for them, and re-layouts: 5.15 us -> 3.47 us
    pallas_call x1, Pallas kernels: 99.1 us -> 96.3 us  [relay_exchange(): pl.pallas_call(functools.partial(relay_kernel, nodes, columns), out_shape...]
    unnamed x6 -> x5, local copies, waits for them, and re-layouts: 3.95 us -> 2.27 us
where the time goes in v2:
time: 162 us
  Pallas kernels  158 us (98%)
  local copies, waits for them, and re-layouts  3.47 us (2%)
    pallas_call x1, Pallas kernels, relay_exchange(): pl.pallas_call(functools.partial(relay_kernel, nodes, columns), out_shape...  96.3 us
    pallas_call x1, Pallas kernels, attention_block(): pl.pallas_call(functools.partial(attention_kernel, lax.axis_size('node'),...  61.7 us

profile of v2, /device:TPU:13, one launch (start us, length us, event | category | flops | bytes accessed | tf_op | source)
XLA Modules:
  0.0 162.1 jit_solution(16651982569728342037)
XLA Ops:
  0.0 0.0 copy-start
  0.0 0.0 copy-start.1
  0.0 61.7 %shard_map.129 = (f32[512,1024]{1,0:T(8,128)}, bf16[512,1024]{1,0:T(8,128)(2,1)S(1)}, f32[512,128]{1,0:T(8,128)S(1)}, f32[8,128]{1,0:T(8,128)}) custom-call(s32[4,8]{1,0:T(4,128)} %neighbour_ref.1, s32[4,8]{1,0:T(4,128)} %live_ref.1, bf16[512,1024]{1,0:T(8,128)(2,1)} %query_hbm.1, bf16[4,128,1024]{2,1,0:T(8,128)(2,1)} %bitcast.15, ...), custom_call_target="tpu_custom_call" | custom-call | tf_op jit(solution)/shard_map/pallas_call | solution.py:272
  61.7 1.2 slice.6
  63.5 0.0 copy-done
  63.5 0.0 copy-done.1
  63.5 96.3 %conditional.1 = (bf16[512,1024]{1,0:T(8,128)(2,1)}) conditional(s32[]{:T(128)} %bitcast.10, (f32[512,128]{1,0:T(8,128)S(1)}, s32[512]{0:T(512)S(1)}, s32[512]{0:T(512)S(1)}, bf16[512,1024]{1,0:T(8,128)(2,1)S(1)}, bf16[1,1024,4096]{2,1,0:T(8,128)(2,1)}, /*index=5*/bf16[1,4096,1024]{2,1,0:T(8,128)(2,1)}, f32[512,1024]{1,0:T(8,128)}) %tuple.20, ...), branch_computations={%region_0.0_spmd, %region_1.0_spmd} | conditional | flops 2151154688 | bytes 8929288 | solution.py:890
  63.6 96.3 %branch_1_fun.1 = bf16[512,1024]{1,0:T(8,128)(2,1)} custom-call(bf16[512,1024]{1,0:T(8,128)(2,1)S(1)} %get-tuple-element.43.normed_ref, f32[512,1024]{1,0:T(8,128)} %get-tuple-element.44.hidden_hbm, f32[512,128]{1,0:T(8,128)S(1)} %get-tuple-element.45.gate_ref, s32[1,512]{1,0:T(1,128)S(1)} %bitcast.19, s32[1,512]{1,0:T(1,128)S(1)} %bitcast.20, ...), custom_call_target="tpu_custom_call" | custom-call | tf_op jit(solution)/shard_map/cond/branch_1_fun/pallas_call | solution.py:787
  159.8 2.3 %copy.20 = bf16[512,1024]{1,0:T(8,128)(2,1)} copy(bf16[512,1024]{1,0:T(8,128)(2,1)} %get-tuple-element.58) | data formatting | bytes 2097152
Async XLA Ops:
  0.0 63.5 %copy-start = (s32[512]{0:T(512)S(1)}, s32[512]{0:T(512)}, u32[]{:S(2)}) copy-start(s32[512]{0:T(512)} %param.24) | copy-start | bytes 6148
  0.0 63.5 %copy-start.1 = (s32[512]{0:T(512)S(1)}, s32[512]{0:T(512)}, u32[]{:S(2)}) copy-start(s32[512]{0:T(512)} %param.25) | copy-start | bytes 6148

commit v3 on v2

--- a/solution.py
+++ b/solution.py
@@ -231,8 +231,8 @@
             preferred_element_type=jnp.float32,
         )
 
-    def finish(t, carry):
-        rows = pl.ds(pl.multiple_of(t * TILE, TILE), TILE)
+    def finish(t):
+        rows = pl.ds(t * TILE, TILE)
         hidden = hidden_ref[rows, :]
         spread = jnp.mean(hidden * hidden, axis=-1, keepdims=True)
         normed = (hidden * lax.rsqrt(spread + 1e-06) * gain_ref[...]).astype(jnp.bfloat16)
@@ -250,11 +250,11 @@
         column = lax.broadcasted_iota(jnp.int32, (TILE, experts), 1).astype(jnp.float32)
         chosen = jnp.sum(jnp.where(wanted == column, logits, 0.0), axis=-1, keepdims=True)
         gate_ref[rows, :] = jnp.broadcast_to(jax.nn.sigmoid(chosen), (TILE, LANES))
-        return carry
-
-    lax.fori_loop(0, tiles, finish, 0)
+
     for copy in second:
         copy.wait_send()
+    for t in range(tiles):
+        finish(t)
 
 
 def attention_block(
@@ -756,15 +756,15 @@
     compute(far, WIDE)
     reply(far)
     repack(far)
+    for g in range(GROUPS):
+        each(g, lambda k: there(g, k, member).wait_send())
+        each(g, lambda k: back(g, k, member).wait_send())
     hidden_copy.wait()
     homeward(near).wait_recv()
     mixed_ref[...] += take_home(near, home_ref[near - 2], fit)
     homeward(far).wait_recv()
     mixed = mixed_ref[...] + take_home(far, home_ref[far - 2], fit)
     out_ref[...] = (hidden_ref[...] + gate_ref[:, 0:1] * mixed).astype(jnp.bfloat16)
-    for g in range(GROUPS):
-        each(g, lambda k: there(g, k, member).wait_send())
-        each(g, lambda k: back(g, k, member).wait_send())
     hop(far).wait_send()
     for g in RELAYED:
         guide(g).wait_send()

time: 162 us -> 160 us (0.988)
  Pallas kernels: 158 us -> 156 us
where the time goes in v3:
time: 160 us
  Pallas kernels  156 us (98%)
  local copies, waits for them, and re-layouts  3.47 us (2%)
    pallas_call x1, Pallas kernels, relay_exchange(): pl.pallas_call(functools.partial(relay_kernel, nodes, columns), out_shape...  95.9 us
    pallas_call x1, Pallas kernels, attention_block(): pl.pallas_call(functools.partial(attention_kernel, lax.axis_size('node'),...  60.1 us

profile of v3, /device:TPU:13, one launch (start us, length us, event | category | flops | bytes accessed | tf_op | source)
XLA Modules:
  0.0 160.2 jit_solution(11493219219478430936)
XLA Ops:
  0.0 0.0 copy-start
  0.0 0.0 copy-start.1
  0.0 60.1 %shard_map.129 = (f32[512,1024]{1,0:T(8,128)}, bf16[512,1024]{1,0:T(8,128)(2,1)S(1)}, f32[512,128]{1,0:T(8,128)S(1)}, f32[8,128]{1,0:T(8,128)}) custom-call(s32[4,8]{1,0:T(4,128)} %neighbour_ref.1, s32[4,8]{1,0:T(4,128)} %live_ref.1, bf16[512,1024]{1,0:T(8,128)(2,1)} %query_hbm.1, bf16[4,128,1024]{2,1,0:T(8,128)(2,1)} %bitcast.15, ...), custom_call_target="tpu_custom_call" | custom-call | tf_op jit(solution)/shard_map/pallas_call | solution.py:272
  60.1 1.2 slice.6
  62.0 0.0 copy-done
  62.0 0.0 copy-done.1
  62.0 95.9 %conditional.1 = (bf16[512,1024]{1,0:T(8,128)(2,1)}) conditional(s32[]{:T(128)} %bitcast.10, (f32[512,128]{1,0:T(8,128)S(1)}, s32[512]{0:T(512)S(1)}, s32[512]{0:T(512)S(1)}, bf16[512,1024]{1,0:T(8,128)(2,1)S(1)}, bf16[1,1024,4096]{2,1,0:T(8,128)(2,1)}, /*index=5*/bf16[1,4096,1024]{2,1,0:T(8,128)(2,1)}, f32[512,1024]{1,0:T(8,128)}) %tuple.20, ...), branch_computations={%region_0.0_spmd, %region_1.0_spmd} | conditional | flops 2151154688 | bytes 8929288 | solution.py:890
  62.0 95.9 %branch_1_fun.1 = bf16[512,1024]{1,0:T(8,128)(2,1)} custom-call(bf16[512,1024]{1,0:T(8,128)(2,1)S(1)} %get-tuple-element.43.normed_ref, f32[512,1024]{1,0:T(8,128)} %get-tuple-element.44.hidden_hbm, f32[512,128]{1,0:T(8,128)S(1)} %get-tuple-element.45.gate_ref, s32[1,512]{1,0:T(1,128)S(1)} %bitcast.19, s32[1,512]{1,0:T(1,128)S(1)} %bitcast.20, ...), custom_call_target="tpu_custom_call" | custom-call | tf_op jit(solution)/shard_map/cond/branch_1_fun/pallas_call | solution.py:787
  157.9 2.3 %copy.20 = bf16[512,1024]{1,0:T(8,128)(2,1)} copy(bf16[512,1024]{1,0:T(8,128)(2,1)} %get-tuple-element.58) | data formatting | bytes 2097152
Async XLA Ops:
  0.0 62.0 %copy-start = (s32[512]{0:T(512)S(1)}, s32[512]{0:T(512)}, u32[]{:S(2)}) copy-start(s32[512]{0:T(512)} %param.24) | copy-start | bytes 6148
  0.0 62.0 %copy-start.1 = (s32[512]{0:T(512)S(1)}, s32[512]{0:T(512)}, u32[]{:S(2)}) copy-start(s32[512]{0:T(512)} %param.25) | copy-start | bytes 6148
